TPU v7x, 32 devices: a whole 2x2x4 slice. The times are simulated.
32 devices in a mesh: dp: 8 (over z, x), feat: 4 (over y, core).
Axes of the slice: x: 2, y: 2, z: 4, core: 2. Of those that a mesh axis runs over, the one named last changes fastest.
Arguments:
- features: float32 [24576, 2048], P('dp', 'feat'), may hold values from -200 to 200
- gamma: float32 [2048], P('feat'), may hold values from 0.5 to 1.5
- beta: float32 [2048], P('feat'), may hold values from -3 to 3
- weight: bfloat16 [2048, 2048], P(None, 'feat'), may hold values from -0.125 to 0.125
- bias: float32 [2048], P('feat'), may hold values from -3 to 3
Outputs:
- activated: float32 [24576, 2048], P('dp', 'feat')
All inputs are finite; a program needn't handle non-finite values.
Results may differ from a plain program's by a relative error of at most 0.0026.
Values may be sent and summed in bfloat16 or wider, within the bound.
No kernel may reach another device: no remote copies, remote signals or barrier semaphores. Data moves between devices by JAX's collectives and lax.ppermute only.
A program may use at most 128 MiB of HBM per device.

v0:
```python
import jax
import jax.numpy as jnp
from jax import lax
from jax.sharding import PartitionSpec as P


def local(features, gamma, beta, weight, bias):
    rows = features.shape[0]
    total_rows = rows * lax.axis_size("dp")
    sums = lax.psum(jnp.sum(features, axis=0), "dp")
    mean = sums / total_rows
    centred_here = features - mean
    devs = lax.psum(jnp.sum(centred_here * centred_here, axis=0), "dp")
    var = devs / total_rows
    scale = gamma / jnp.sqrt(var + 1e-05)
    normed = ((features - mean) * scale + beta).astype(jnp.bfloat16)
    product = jnp.dot(
        lax.all_gather(normed, "feat", axis=1, tiled=True),
        weight,
        preferred_element_type=jnp.float32,
    )
    return jnp.maximum(product + bias, 0.0)


def solution(mesh):
    placed = (P("dp", "feat"), P("feat"), P("feat"), P(None, "feat"), P("feat"))
    return jax.shard_map(
        local, mesh=mesh, in_specs=placed, out_specs=P("dp", "feat"), check_vma=False
    )
```

profile of v0, /device:TPU:0, one launch (start us, length us, event | category | flops | bytes accessed | tf_op | source)
XLA Modules:
  0.0 158.3 jit_solution(14574581504709749969)
XLA Ops:
  6.5 0.0 copy-start
  6.5 0.0 copy-start.2
  6.5 0.0 copy-start.1
  6.5 0.0 all-gather.2.cloned.1.call-start
  6.5 3.4 %reduce_sum.18 = f32[512]{0:T(512)S(1)} reduce(f32[3072,512]{1,0:T(8,128)} %param.5, f32[]{:T(128)} %constant.3.clone.1), dimensions={0}, to_apply=%region_0.0 | reduce | flops 1572352 | bytes 6293508 | tf_op jit(solution)/shard_map/reduce_sum | solution.py:10
  9.9 23.1 %psum.14 = f32[512]{0:T(512)S(1)} all-reduce(f32[512]{0:T(512)S(1)} %reduce_sum.18), channel_id=1, replica_groups=mesh['dp'=8,'feat'=4] {'dp'}, use_global_device_ids=true, to_apply=%region_1.0 | all-reduce | flops 512 | bytes 4096 | tf_op jit(solution)/shard_map/psum | solution.py:10
  33.1 3.5 %multiply_reduce_fusion = f32[512]{0:T(512)S(1)} fusion(f32[3072,512]{1,0:T(8,128)} %param.5, f32[512]{0:T(512)S(1)} %broadcast_multiply_fusion), kind=kLoop, calls=%fused_computation.2 | loop fusion | flops 4718080 | bytes 6295552 | tf_op jit(solution)/shard_map/reduce_sum | solution.py:13
  36.6 17.1 %psum.15 = f32[512]{0:T(512)S(1)} all-reduce(f32[512]{0:T(512)S(1)} %multiply_reduce_fusion), channel_id=1, replica_groups=mesh['dp'=8,'feat'=4] {'dp'}, use_global_device_ids=true, to_apply=%region_3.0 | all-reduce | flops 512 | bytes 4096 | tf_op jit(solution)/shard_map/psum | solution.py:13
  53.7 0.0 copy-done.2
  53.7 0.0 copy-done.1
  53.7 0.0 copy-start.3
  53.7 5.4 %add_convert_fusion = bf16[3072,512]{1,0:T(8,128)(2,1)} fusion(f32[3072,512]{1,0:T(8,128)} %param.5, f32[512]{0:T(512)S(1)} %copy-done.1, f32[512]{0:T(512)S(1)} %rsqrt_multiply_fusion, f32[512]{0:T(512)S(1)} %broadcast_multiply_fusion), kind=kLoop, calls=%fused_computation.1 | loop fusion | flops 6291456 | bytes 9443328 | tf_op jit(solution)/shard_map/convert_element_type | solution.py:16
  59.1 0.0 all-gather.2.cloned.1.call-update
  59.1 81.0 %all-gather.2.cloned.1.call-done = bf16[3072,2048]{1,0:T(8,128)(2,1)} async-done(((bf16[3072,512]{1,0:T(8,128)(2,1)}), bf16[3072,2048]{1,0:T(8,128)(2,1)}) %all-gather.2.cloned.1.call-update) | async-done | bytes 12582928 | tf_op jit(solution)/shard_map/all_gather | solution.py:18
  140.1 0.0 copy-done
  140.1 0.0 copy-done.3
  140.1 11.3 %add_maximum_fusion = f32[3072,512]{1,0:T(8,128)} fusion(bf16[3072,2048]{1,0:T(8,128)(2,1)} %all-gather.2.cloned.1.call-done, bf16[2048,512]{1,0:T(8,128)(2,1)S(1)} %copy-done, f32[512]{0:T(512)S(1)} %copy-done.3), kind=kOutput, calls=%fused_computation | convolution fusion | flops 6445596672 | bytes 20973568 | tf_op jit(solution)/shard_map/dot_general | solution.py:17
  (2 shorter events, 0.0 us)
Async XLA Ops:
  6.5 133.6 %copy-start = (bf16[2048,512]{1,0:T(8,128)(2,1)S(1)}, bf16[2048,512]{1,0:T(8,128)(2,1)}, u32[]{:S(2)}) copy-start(bf16[2048,512]{1,0:T(8,128)(2,1)} %param.8) | copy-start | bytes 6291460
  6.5 47.2 %copy-start.2 = (f32[512]{0:T(512)S(1)}, f32[512]{0:T(512)}, u32[]{:S(2)}) copy-start(f32[512]{0:T(512)} %param.6) | copy-start | bytes 6148
  6.5 47.2 %copy-start.1 = (f32[512]{0:T(512)S(1)}, f32[512]{0:T(512)}, u32[]{:S(2)}) copy-start(f32[512]{0:T(512)} %param.7) | copy-start | bytes 6148
  6.5 133.6 %all-gather.2.cloned.1.call-start = ((), (), s32[]{:S(2)}) async-start(), calls=%async_computation | async-start | bytes 15728640 | tf_op jit(solution)/shard_map/all_gather | solution.py:18
  53.7 86.4 %copy-start.3 = (f32[512]{0:T(512)S(1)}, f32[512]{0:T(512)}, u32[]{:S(2)}) copy-start(f32[512]{0:T(512)} %param.9) | copy-start | bytes 6148
Sparse Core Ops, SparseCore 0:
  59.3 80.8 all-gather.1
where the time goes:
time: 159 us; the launch traced here: 158 us
  waiting for transfers between devices  81 us (51%)
  blocking collectives  40.2 us (25%)
  between operations  13.4 us (8%)
  other arithmetic  12.3 us (8%)
  matrix products  11.3 us (7%)
    all_gather x1, waiting for transfers between devices, local(): lax.all_gather(normed, 'feat', axis=1, tiled=True)  81 us
    psum x1, blocking collectives, local(): sums = lax.psum(jnp.sum(features, axis=0), 'dp')  23.1 us
    psum x1, blocking collectives, local(): devs = lax.psum(jnp.sum(centred_here * centred_here, axis=0), 'dp')  17.1 us
    dot_general x1, matrix products, local(): jnp.dot(lax.all_gather(normed, 'feat', axis=1, tiled=True), weight, prefe...  11.3 us
    convert_element_type x1, other arithmetic, local(): normed = ((features - mean) * scale + beta).astype(jnp.bfloat16)  5.36 us
    reduce_sum x1, other arithmetic, local(): devs = lax.psum(jnp.sum(centred_here * centred_here, axis=0), 'dp')  3.52 us
    reduce_sum x1, other arithmetic, local(): sums = lax.psum(jnp.sum(features, axis=0), 'dp')  3.4 us
  transfers between devices with their start and end apart: 1, of which 1 were waited for; matrix products, arithmetic and copies ran while one was open for 0% of the time, Pallas kernels for 0%

commit v1 on v0

--- a/solution.py
+++ b/solution.py
@@ -2,6 +2,12 @@
 import jax.numpy as jnp
 from jax import lax
 from jax.sharding import PartitionSpec as P
+
+
+def gather_and_add(block, name):
+    shards = lax.all_gather(block, name, axis=0, tiled=False)
+    summed = shards.sum(axis=0)
+    return summed
 
 
 def local(features, gamma, beta, weight, bias):
@@ -10,7 +16,7 @@
     sums = lax.psum(jnp.sum(features, axis=0), "dp")
     mean = sums / total_rows
     centred_here = features - mean
-    devs = lax.psum(jnp.sum(centred_here * centred_here, axis=0), "dp")
+    devs = gather_and_add(jnp.sum(centred_here * centred_here, axis=0), "dp")
     var = devs / total_rows
     scale = gamma / jnp.sqrt(var + 1e-05)
     normed = ((features - mean) * scale + beta).astype(jnp.bfloat16)

time: 159 us -> 166 us (1.044)
  blocking collectives: 40.2 us -> 49.2 us
    all_gather x0 -> x1, blocking collectives: none -> 26.1 us  [gather_and_add(): shards = lax.all_gather(block, name, axis=0, tiled=False)]
    psum x1 -> x0, blocking collectives: 17.1 us -> none  [local(): devs = lax.psum(jnp.sum(centred_here * centred_here, axis=0), 'dp')]
    reduce_sum x1 -> x2, other arithmetic: 3.52 us -> 3.55 us  [the longest x1 3.52 us: local(): devs = gather_and_add(jnp.sum(centred_here * centred_here, axis=0), 'dp')]
where the time goes in v1:
time: 166 us
  waiting for transfers between devices  79.5 us (48%)
  blocking collectives  49.2 us (30%)
  between operations  13.4 us (8%)
  other arithmetic  12.3 us (7%)
  matrix products  11.3 us (7%)
    all_gather x1, waiting for transfers between devices, local(): lax.all_gather(normed, 'feat', axis=1, tiled=True)  79.5 us
    all_gather x1, blocking collectives, gather_and_add(): shards = lax.all_gather(block, name, axis=0, tiled=False)  26.1 us
    psum x1, blocking collectives, local(): sums = lax.psum(jnp.sum(features, axis=0), 'dp')  23.1 us
    dot_general x1, matrix products, local(): jnp.dot(lax.all_gather(normed, 'feat', axis=1, tiled=True), weight, prefe...  11.3 us
    convert_element_type x1, other arithmetic, local(): normed = ((features - mean) * scale + beta).astype(jnp.bfloat16)  5.36 us
    reduce_sum x1, other arithmetic, local(): devs = gather_and_add(jnp.sum(centred_here * centred_here, axis=0), 'dp')  3.52 us
    reduce_sum x1, other arithmetic, local(): sums = lax.psum(jnp.sum(features, axis=0), 'dp')  3.4 us
  transfers between devices with their start and end apart: 1, of which 1 were waited for; matrix products, arithmetic and copies ran while one was open for 0% of the time, Pallas kernels for 0%

profile of v1, /device:TPU:0, one launch (start us, length us, event | category | flops | bytes accessed | tf_op | source)
XLA Modules:
  0.0 165.9 jit_solution(11281098698904760288)
XLA Ops:
  6.5 0.0 copy-start
  6.5 0.0 copy-start.2
  6.5 0.0 copy-start.1
  6.5 0.0 all-gather.4.cloned.1.call-start
  6.5 3.4 %reduce_sum.27 = f32[512]{0:T(512)S(1)} reduce(f32[3072,512]{1,0:T(8,128)} %param.5, f32[]{:T(128)} %constant.3.clone.1), dimensions={0}, to_apply=%region_0.0 | reduce | flops 1572352 | bytes 6293508 | tf_op jit(solution)/shard_map/reduce_sum | solution.py:16
  9.9 23.1 %psum.7 = f32[512]{0:T(512)S(1)} all-reduce(f32[512]{0:T(512)S(1)} %reduce_sum.27), channel_id=1, replica_groups=mesh['dp'=8,'feat'=4] {'dp'}, use_global_device_ids=true, to_apply=%region_1.0 | all-reduce | flops 512 | bytes 4096 | tf_op jit(solution)/shard_map/psum | solution.py:16
  33.1 3.5 %multiply_reduce_fusion = f32[512]{0:T(512)S(1)} fusion(f32[3072,512]{1,0:T(8,128)} %param.5, f32[512]{0:T(512)S(1)} %broadcast_multiply_fusion), kind=kLoop, calls=%fused_computation.2 | loop fusion | flops 4718080 | bytes 6295552 | tf_op jit(solution)/shard_map/reduce_sum | solution.py:19
  36.6 26.1 %all-gather.1 = f32[8,1,512]{2,1,0:T(1,128)S(1)} all-gather(f32[1,1,512]{2,1,0:T(1,128)S(1)} %bitcast.3), channel_id=2, replica_groups=mesh['dp'=8,'feat'=4] {'dp'}, dimensions={0}, use_global_device_ids=true | all-gather | bytes 18432 | tf_op jit(solution)/shard_map/all_gather | solution.py:8
  62.7 0.0 copy-done.2
  62.8 0.0 copy-done.1
  62.8 0.0 copy-start.3
  62.8 5.4 %add_convert_fusion = bf16[3072,512]{1,0:T(8,128)(2,1)} fusion(f32[3072,512]{1,0:T(8,128)} %param.5, f32[512]{0:T(512)S(1)} %copy-done.1, f32[512]{0:T(512)S(1)} %rsqrt_multiply_fusion, f32[512]{0:T(512)S(1)} %broadcast_multiply_fusion), kind=kLoop, calls=%fused_computation.1 | loop fusion | flops 6291456 | bytes 9443328 | tf_op jit(solution)/shard_map/convert_element_type | solution.py:22
  68.1 0.0 all-gather.4.cloned.1.call-update
  68.2 79.5 %all-gather.4.cloned.1.call-done = bf16[3072,2048]{1,0:T(8,128)(2,1)} async-done(((bf16[3072,512]{1,0:T(8,128)(2,1)}), bf16[3072,2048]{1,0:T(8,128)(2,1)}) %all-gather.4.cloned.1.call-update) | async-done | bytes 12582928 | tf_op jit(solution)/shard_map/all_gather | solution.py:24
  147.7 0.0 copy-done
  147.7 0.0 copy-done.3
  147.7 11.3 %add_maximum_fusion = f32[3072,512]{1,0:T(8,128)} fusion(bf16[3072,2048]{1,0:T(8,128)(2,1)} %all-gather.4.cloned.1.call-done, bf16[2048,512]{1,0:T(8,128)(2,1)S(1)} %copy-done, f32[512]{0:T(512)S(1)} %copy-done.3), kind=kOutput, calls=%fused_computation | convolution fusion | flops 6445596672 | bytes 20973568 | tf_op jit(solution)/shard_map/dot_general | solution.py:23
  (3 shorter events, 0.0 us)
Async XLA Ops:
  6.5 141.2 %copy-start = (bf16[2048,512]{1,0:T(8,128)(2,1)S(1)}, bf16[2048,512]{1,0:T(8,128)(2,1)}, u32[]{:S(2)}) copy-start(bf16[2048,512]{1,0:T(8,128)(2,1)} %param.8) | copy-start | bytes 6291460
  6.5 56.2 %copy-start.2 = (f32[512]{0:T(512)S(1)}, f32[512]{0:T(512)}, u32[]{:S(2)}) copy-start(f32[512]{0:T(512)} %param.6) | copy-start | bytes 6148
  6.5 56.2 %copy-start.1 = (f32[512]{0:T(512)S(1)}, f32[512]{0:T(512)}, u32[]{:S(2)}) copy-start(f32[512]{0:T(512)} %param.7) | copy-start | bytes 6148
  6.5 141.1 %all-gather.4.cloned.1.call-start = ((), (), s32[]{:S(2)}) async-start(), calls=%async_computation | async-start | bytes 15728640 | tf_op jit(solution)/shard_map/all_gather | solution.py:24
  62.8 84.9 %copy-start.3 = (f32[512]{0:T(512)S(1)}, f32[512]{0:T(512)}, u32[]{:S(2)}) copy-start(f32[512]{0:T(512)} %param.9) | copy-start | bytes 6148
Sparse Core Ops, SparseCore 0:
  68.3 79.3 all-gather.3
